TPU v7x, 32 devices: a whole 2x2x4 slice. The times are simulated.
32 devices in a mesh: fsdp: 16 (over z, y, core), grp: 2 (over x).
Axes of the slice: x: 2, y: 2, z: 4, core: 2. Of those that a mesh axis runs over, the one named last changes fastest.
Arguments:
- hidden: bfloat16 [8192, 3072], P('fsdp', 'grp'), may hold values from -16 to 16
- queries: bfloat16 [8192, 1536], P('fsdp', 'grp'), may hold values from -6 to 6
- attn_keys: bfloat16 [8192, 1536], P('fsdp', 'grp'), may hold values from -6 to 6
- w_value: bfloat16 [1536, 3072], P('fsdp', 'grp'), may hold values from -1 to 1
- w_out: bfloat16 [1536, 3072], P('fsdp', 'grp'), may hold values from -1 to 1
- alpha: float32 [3072], P('grp'), may hold values from 0.05 to 0.5
- out_grad: bfloat16 [8192, 3072], P('fsdp', 'grp'), may hold values from -6 to 6
Outputs:
- new_hidden: bfloat16 [8192, 3072], P('fsdp', 'grp')
- grad_hidden: bfloat16 [8192, 3072], P('fsdp', 'grp')
- grad_queries: bfloat16 [8192, 1536], P('fsdp', 'grp')
- grad_keys: bfloat16 [8192, 1536], P('fsdp', 'grp')
- grad_w_value: float32 [1536, 3072], P('fsdp', 'grp')
- grad_w_out: float32 [1536, 3072], P('fsdp', 'grp')
All inputs are finite; a program needn't handle non-finite values.
Results may differ from a plain program's by a relative error of at most 0.012.
The roundings to bfloat16 on the way count: a program that leaves them out, or rounds other values in their place, can miss the bound.
Values may be sent and summed in bfloat16 or wider, within the bound.
A program may use at most 192 MiB of HBM per device.

v0:
```python
import jax
import jax.numpy as jnp
from jax import lax
from jax.sharding import PartitionSpec as P

D = 3072
HS = 128
EPS = 1e-06


def contract_last(left, right):
    return lax.dot_general(
        left, right, (((1,), (1,)), ((), ())), preferred_element_type=jnp.float32
    )


def contract_first(left, right):
    return lax.dot_general(
        left, right, (((0,), (0,)), ((), ())), preferred_element_type=jnp.float32
    )


def causal_probs(query_head, key_head):
    length = query_head.shape[0]
    score_scale = query_head.shape[1] ** (-0.5)
    scores = contract_last(query_head, key_head) * score_scale
    row_pos = lax.broadcasted_iota(jnp.int32, (length, length), 0)
    col_pos = lax.broadcasted_iota(jnp.int32, (length, length), 1)
    scores = jnp.where(row_pos >= col_pos, scores, -1e30)
    row_peak = jnp.max(scores, axis=1, keepdims=True)
    exp_terms = jnp.exp(scores - row_peak)
    return exp_terms / jnp.sum(exp_terms, axis=1, keepdims=True)


def head_forward(items):
    query_head, key_head, value_head = items
    attn_prob = causal_probs(query_head, key_head)
    return jnp.dot(
        attn_prob.astype(jnp.bfloat16), value_head, preferred_element_type=jnp.float32
    ).astype(jnp.bfloat16)


def head_backward(items):
    query_head, key_head, value_head, grad_head = items
    score_scale = query_head.shape[1] ** (-0.5)
    attn_prob = causal_probs(query_head, key_head)
    prob_half = attn_prob.astype(jnp.bfloat16)
    grad_prob = contract_last(grad_head, value_head)
    row_delta = jnp.sum(attn_prob * grad_prob, axis=1, keepdims=True)
    grad_score = (attn_prob * (grad_prob - row_delta)).astype(jnp.bfloat16)
    grad_query = (
        jnp.dot(grad_score, key_head, preferred_element_type=jnp.float32) * score_scale
    ).astype(jnp.bfloat16)
    grad_key = (contract_first(grad_score, query_head) * score_scale).astype(jnp.bfloat16)
    grad_value = contract_first(prob_half, grad_head).astype(jnp.bfloat16)
    return (grad_query, grad_key, grad_value)


def split_heads(block):
    return block.reshape(block.shape[0], -1, HS).transpose(1, 0, 2)


def join_heads(stacked):
    return stacked.transpose(1, 0, 2).reshape(stacked.shape[1], -1)


def shards(hidden, queries, attn_keys, w_value, w_out, alpha, out_grad):
    half_width = hidden.shape[1]
    value_rows = w_value.astype(jnp.float32)
    out_rows = w_out.astype(jnp.float32)
    row_sums = lax.psum(
        (jnp.sum(value_rows * value_rows, axis=1), jnp.sum(out_rows * out_rows, axis=1)), "grp"
    )
    norm_v = jnp.sqrt(row_sums[0] + EPS)[:, None]
    norm_o = jnp.sqrt(row_sums[1] + EPS)[:, None]
    unit_v = value_rows / norm_v
    unit_o = out_rows / norm_o
    weight_v, weight_o = (
        lax.all_gather(unit_v.astype(jnp.bfloat16), "fsdp", axis=0, tiled=True),
        lax.all_gather(unit_o.astype(jnp.bfloat16), "fsdp", axis=0, tiled=True),
    )
    value_parts = contract_last(hidden, weight_v)
    values_mine = lax.psum_scatter(value_parts, "grp", scatter_dimension=1, tiled=True).astype(
        jnp.bfloat16
    )
    q_heads = split_heads(queries)
    k_heads = split_heads(attn_keys)
    v_heads = split_heads(values_mine)
    attn_mine = join_heads(lax.map(head_forward, (q_heads, k_heads, v_heads)))
    attn_all = lax.all_gather(attn_mine, "grp", axis=1, tiled=True)
    proj = jnp.dot(attn_all, weight_o, preferred_element_type=jnp.float32)
    hidden_f = hidden.astype(jnp.float32)
    keep_rate = 1.0 - alpha
    moments = lax.psum(
        (
            jnp.sum(proj * proj, axis=1),
            jnp.sum(keep_rate * keep_rate * hidden_f * hidden_f, axis=1),
            jnp.sum(keep_rate * alpha * hidden_f * proj, axis=1),
            jnp.sum(alpha * alpha * proj * proj, axis=1),
        ),
        "grp",
    )
    proj_rs = lax.rsqrt(moments[0] / D + EPS)[:, None]
    cross_sum = moments[2][:, None]
    alpha_sum = moments[3][:, None]
    mix_mean = (moments[1][:, None] + 2.0 * proj_rs * cross_sum + proj_rs * proj_rs * alpha_sum) / D
    mix_rs = lax.rsqrt(mix_mean + EPS)
    mixed = hidden_f + alpha * (proj * proj_rs - hidden_f)
    new_hidden = (mixed * mix_rs).astype(jnp.bfloat16)
    grad_out = out_grad.astype(jnp.float32)
    grad_sums = lax.psum(
        (
            jnp.sum(grad_out * keep_rate * hidden_f, axis=1),
            jnp.sum(grad_out * alpha * proj, axis=1),
        ),
        "grp",
    )
    grad_mean = (grad_sums[0][:, None] + proj_rs * grad_sums[1][:, None]) / D
    grad_mix = mix_rs * (grad_out - mixed * mix_rs * mix_rs * grad_mean)
    grad_pn = grad_mix * alpha
    proj_mean = (
        mix_rs * grad_sums[1][:, None]
        - mix_rs * mix_rs * mix_rs * grad_mean * (cross_sum + proj_rs * alpha_sum)
    ) / D
    grad_res = grad_mix * keep_rate
    grad_proj = proj_rs * (grad_pn - proj * proj_rs * proj_rs * proj_mean)
    grad_proj_b = grad_proj.astype(jnp.bfloat16)
    grad_attn_parts = contract_last(grad_proj_b, weight_o)
    grad_attn = lax.psum_scatter(grad_attn_parts, "grp", scatter_dimension=1, tiled=True).astype(
        jnp.bfloat16
    )
    grad_q, grad_k, grad_v = lax.map(
        head_backward, (q_heads, k_heads, v_heads, split_heads(grad_attn))
    )
    grad_values = lax.all_gather(join_heads(grad_v), "grp", axis=1, tiled=True)
    grad_hidden = (
        grad_res + jnp.dot(grad_values, weight_v, preferred_element_type=jnp.float32)
    ).astype(jnp.bfloat16)
    owned = lax.psum_scatter(
        jnp.concatenate(
            (contract_first(grad_values, hidden), contract_first(attn_all, grad_proj_b)), axis=1
        ),
        "fsdp",
        scatter_dimension=0,
        tiled=True,
    )
    gw_v_own = owned[:, :half_width]
    gw_o_own = owned[:, half_width:]
    row_dot = lax.psum(
        (jnp.sum(gw_v_own * unit_v, axis=1), jnp.sum(gw_o_own * unit_o, axis=1)), "grp"
    )
    grad_w_value = (gw_v_own - unit_v * row_dot[0][:, None]) / norm_v
    grad_w_out = (gw_o_own - unit_o * row_dot[1][:, None]) / norm_o
    return (
        new_hidden,
        grad_hidden,
        join_heads(grad_q),
        join_heads(grad_k),
        grad_w_value,
        grad_w_out,
    )


def solution(mesh):
    placed = (
        P("fsdp", "grp"),
        P("fsdp", "grp"),
        P("fsdp", "grp"),
        P("fsdp", "grp"),
        P("fsdp", "grp"),
        P("grp"),
        P("fsdp", "grp"),
    )
    return jax.shard_map(
        shards,
        mesh=mesh,
        in_specs=placed,
        out_specs=(
            P("fsdp", "grp"),
            P("fsdp", "grp"),
            P("fsdp", "grp"),
            P("fsdp", "grp"),
            P("fsdp", "grp"),
            P("fsdp", "grp"),
        ),
        check_vma=False,
    )
```

profile of v0, /device:TPU:0, one launch (start us, length us, event | category | flops | bytes accessed | tf_op | source)
XLA Modules:
  0.0 593.8 jit_solution(14473532207321060292)
XLA Ops:
  8.5 5.9 all-reduce.2
  14.4 1.8 fusion.60
  16.2 55.0 %all-gather.5.cloned.1.call-done = bf16[1536,1536]{1,0:T(8,128)(2,1)} async-done(((bf16[96,1536]{1,0:T(8,128)(2,1)}), bf16[1536,1536]{1,0:T(8,128)(2,1)}) %all-gather.5.cloned.1.call-update) | async-done | bytes 4718608 | tf_op jit(solution)/shard_map/all_gather | solution.py:79
  71.3 7.1 %convolution_bitcast_fusion = f32[512,1536]{0,1:T(8,128)} fusion(bf16[1536,1536]{1,0:T(8,128)(2,1)} %all-gather.5.cloned.1.call-done, bf16[512,1536]{1,0:T(8,128)(2,1)} %param.11), kind=kOutput, calls=%fused_computation.68 | convolution fusion | flops 2415919104 | bytes 9437184 | tf_op jit(solution)/shard_map/dot_general | solution.py:12
  81.6 39.0 %reduce-scatter.6.cloned.1.call-done = f32[512,768]{0,1:T(8,128)} async-done(((f32[512,1536]{0,1:T(8,128)}), f32[512,768]{0,1:T(8,128)}) %reduce-scatter.6.cloned.1.call-update) | async-done | bytes 1572880 | tf_op jit(solution)/shard_map/reduce_scatter | solution.py:83
  120.6 1.5 convert_element_type.57
  123.3 11.8 %while.24 = (s32[]{:T(128)}, bf16[6,512,128]{1,2,0:T(8,128)(2,1)S(1)}, bf16[6,512,128]{2,1,0:T(8,128)(2,1)S(1)}, bf16[6,512,128]{2,1,0:T(8,128)(2,1)S(1)}, bf16[6,512,128]{2,1,0:T(8,128)(2,1)}, /*index=5*/s32[]{:T(128)}) while((s32[]{:T(128)}, bf16[6,512,128]{1,2,0:T(8,128)(2,1)S(1)}, bf16[6,512,128]{2,1,0:T(8,128)(2,1)S(1)}, ...), condition=%wide.region_6.7_spmd, body=%wide.region_3.6_spmd.sunk | while | flops 136641536 | bytes 4205653 | solution.py:89
  123.8 1.3 fusion.100
  125.8 1.3 fusion.100
  127.8 1.3 fusion.100
  129.7 1.3 fusion.100
  131.7 1.3 fusion.100
  133.7 1.3 fusion.100
  136.1 40.5 %all-gather.9.cloned.1.call-done = bf16[1536,1536]{1,0:T(8,128)(2,1)} async-done(((bf16[96,1536]{1,0:T(8,128)(2,1)}), bf16[1536,1536]{1,0:T(8,128)(2,1)}) %all-gather.9.cloned.1.call-update) | async-done | bytes 4718608 | tf_op jit(solution)/shard_map/all_gather | solution.py:80
  176.6 27.7 %all-gather.7.cloned.1.call-done = bf16[512,1536]{0,1:T(8,128)(2,1)} async-done(((bf16[512,768]{0,1:T(8,128)(2,1)}), bf16[512,1536]{0,1:T(8,128)(2,1)}) %all-gather.7.cloned.1.call-update) | async-done | bytes 1572880 | tf_op jit(solution)/shard_map/all_gather | solution.py:90
  204.3 8.4 %fusion.43 = (f32[512]{0:T(512)S(1)}, f32[512]{0:T(512)S(1)}, f32[512]{0:T(512)S(1)}, f32[512]{0:T(512)S(1)}, f32[512]{0:T(512)S(1)}, /*index=5*/f32[512]{0:T(512)S(1)}, f32[512,1536]{1,0:T(8,128)S(1)}) fusion(bf16[512,1536]{1,0:T(8,128)(2,1)} %param.17, f32[1536]{0:T(1024)S(1)} %copy-done.14, f32[1536]{0:T(1024)S(1)} %get-tuple-element.182, ...), kind=kOutput, calls=%fused_computation.72 | convolution fusion | flops 2430858240 | bytes 12625920 | tf_op jit(solution)/shard_map/dot_general | solution.py:91
  212.7 6.9 %all-reduce.1 = (f32[512]{0:T(512)S(1)}, f32[512]{0:T(512)S(1)}, f32[512]{0:T(512)S(1)}, f32[512]{0:T(512)S(1)}, f32[512]{0:T(512)S(1)}, /*index=5*/f32[512]{0:T(512)S(1)}) all-reduce(f32[512]{0:T(512)S(1)} %get-tuple-element.126, f32[512]{0:T(512)S(1)} %get-tuple-element.130, ...), channel_id=1, replica_groups=mesh['fsdp'=16,'grp'=2] {'grp'}, use_global_device_ids=true, to_apply=%region_16.17 | all-reduce | flops 3072 | bytes 24576 | tf_op jit(solution)/shard_map/psum | solution.py:94
  219.7 4.5 multiply_convert_fusion.1
  225.4 4.3 fusion.65
  229.7 44.7 %reduce-scatter.8.cloned.1.call-done = f32[512,768]{1,0:T(8,128)} async-done(((f32[512,1536]{1,0:T(8,128)}), f32[512,768]{1,0:T(8,128)}) %reduce-scatter.8.cloned.1.call-update) | async-done | bytes 1572880 | tf_op jit(solution)/shard_map/reduce_scatter | solution.py:129
  274.5 1.5 convert_element_type.63
  278.2 47.0 %while.25 = (s32[]{:T(128)}, bf16[6,512,128]{1,2,0:T(8,128)(2,1)}, bf16[6,512,128]{1,2,0:T(8,128)(2,1)S(1)}, bf16[6,512,128]{1,2,0:T(8,128)(2,1)S(1)}, bf16[6,51...) while((s32[]{:T(128)}, bf16[6,512,128]{1,2,0:T(8,128)(2,1)}, ...), condition=%wide.region_26.27_spmd, body=%wide.region_22.26_spmd.sunk | while | flops 340589056 | bytes 11821177 | solution.py:132
  278.2 1.3 fusion.107
  281.0 1.3 multiply_reduce_fusion.5
  286.0 1.3 fusion.107
  288.9 1.3 multiply_reduce_fusion.5
  293.9 1.3 fusion.107
  296.7 1.3 multiply_reduce_fusion.5
  299.5 1.3 fusion.109
  301.7 1.3 fusion.107
  304.6 1.3 multiply_reduce_fusion.5
  307.4 1.3 fusion.109
  309.6 1.3 fusion.107
  312.4 1.3 multiply_reduce_fusion.5
  315.2 1.3 fusion.109
  317.4 1.3 fusion.107
  320.3 1.3 multiply_reduce_fusion.5
  323.0 1.3 fusion.109
  326.2 8.5 %fusion.67 = f32[1536,1536]{0,1:T(8,128)} fusion(bf16[512,1536]{0,1:T(8,128)(2,1)} %all-gather.7.cloned.1.call-done, bf16[512,1536]{1,0:T(8,128)(2,1)} %copy-done.11), kind=kOutput, calls=%fused_computation.114 | convolution fusion | flops 2415919104 | bytes 12582912 | tf_op jit(solution)/shard_map/dot_general | solution.py:18
  334.7 18.8 %all-gather.11.cloned.1.call-done = bf16[512,1536]{0,1:T(8,128)(2,1)} async-done(((bf16[512,768]{0,1:T(8,128)(2,1)}), bf16[512,1536]{0,1:T(8,128)(2,1)}) %all-gather.11.cloned.1.call-update) | async-done | bytes 1572880 | tf_op jit(solution)/shard_map/all_gather | solution.py:135
  353.5 4.2 fusion.66
  357.8 7.2 %pad_maximum_fusion = f32[1536,3072]{0,1:T(8,128)} fusion(f32[1536,1536]{0,1:T(8,128)S(1)} %copy-done, f32[1536,1536]{0,1:T(8,128)S(1)} %fusion.66), kind=kLoop, calls=%fused_computation.57 | loop fusion | flops 4718592 | bytes 37748736 | tf_op jit(solution)/shard_map/concatenate | solution.py:140
  365.0 18.7 %copy.57 = f32[1536,3072]{1,0:T(8,128)} copy(f32[1536,3072]{0,1:T(8,128)} %pad_maximum_fusion) | data formatting | bytes 37748736
  387.1 9.9 %fusion.51 = bf16[512,1536]{1,0:T(8,128)(2,1)} fusion(bf16[512,1536]{0,1:T(8,128)(2,1)} %all-gather.11.cloned.1.call-done, bf16[1536,1536]{1,0:T(8,128)(2,1)} %all-gather.5.cloned.1.call-done, bf16[512,1536]{1,0:T(8,128)(2,1)S(1)} %copy-done.9, f32[512]{0:T(512)S(1)} %get-tuple-element.187, f32[1536]{0:T(1024)S(1)} %get-tuple-element.185, ...), kind=kOutput, calls=%fused_computation.82 | convolution fusion | flops 2426929152 | bytes 14174208 | tf_op jit(solution)/shard_map/dot_general | solution.py:137
  397.0 180.8 %reduce-scatter.10.cloned.1.call-done = f32[96,3072]{1,0:T(8,128)} async-done(((f32[1536,3072]{1,0:T(8,128)}), f32[96,3072]{1,0:T(8,128)}) %reduce-scatter.10.cloned.1.call-update) | async-done | bytes 1179664 | tf_op jit(solution)/shard_map/reduce_scatter | solution.py:139
  577.9 1.6 multiply_reduce_fusion.2
  579.5 4.9 all-reduce
  584.4 2.5 subtract_divide_fusion
  (144 shorter events, 44.6 us)
Async XLA Ops:
  7.2 64.1 %all-gather.5.cloned.1.call-start = ((), (), s32[]{:S(2)}) async-start(), calls=%async_computation.3 | async-start | bytes 5013504 | tf_op jit(solution)/shard_map/all_gather | solution.py:79
  16.2 104.4 %reduce-scatter.6.cloned.1.call-start = ((), (), s32[]{:S(2)}) async-start(), calls=%async_computation.4 | async-start | bytes 4718592 | tf_op jit(solution)/shard_map/reduce_scatter | solution.py:83
  78.4 1.0 copy-start.2
  78.4 1.9 copy-start.12
  78.4 2.5 copy-start.13
  78.4 98.1 %all-gather.9.cloned.1.call-start = ((), (), s32[]{:S(2)}) async-start(), calls=%async_computation.6 | async-start | bytes 5013504 | tf_op jit(solution)/shard_map/all_gather | solution.py:80
  80.2 124.1 %all-gather.7.cloned.1.call-start = ((), (), s32[]{:S(2)}) async-start(), calls=%async_computation.5 | async-start | bytes 2359296 | tf_op jit(solution)/shard_map/all_gather | solution.py:90
  123.3 12.8 %copy-start.14 = (f32[1536]{0:T(1024)S(1)}, f32[1536]{0:T(1024)}, u32[]{:S(2)}) copy-start(f32[1536]{0:T(1024)} %param.16) | copy-start | bytes 18436
  135.1 0.9 copy-start.5
  135.1 69.2 %copy-start.7 = (bf16[6,512,128]{2,1,0:T(8,128)(2,1)}, bf16[6,512,128]{2,1,0:T(8,128)(2,1)S(1)}, u32[]{:S(2)}) copy-start(bf16[6,512,128]{2,1,0:T(8,128)(2,1)S(1)} %get-tuple-element.351) | copy-start | bytes 2359300
  135.1 69.2 %copy-start.8 = (bf16[6,512,128]{2,1,0:T(8,128)(2,1)}, bf16[6,512,128]{2,1,0:T(8,128)(2,1)S(1)}, u32[]{:S(2)}) copy-start(bf16[6,512,128]{2,1,0:T(8,128)(2,1)S(1)} %get-tuple-element.352) | copy-start | bytes 2359300
  136.0 138.4 %reduce-scatter.8.cloned.1.call-start = ((), (), s32[]{:S(2)}) async-start(), calls=%async_computation.7 | async-start | bytes 4718592 | tf_op jit(solution)/shard_map/reduce_scatter | solution.py:129
  212.7 11.5 %copy-start.6 = (f32[512,1536]{1,0:T(8,128)}, f32[512,1536]{1,0:T(8,128)S(1)}, u32[]{:S(2)}) copy-start(f32[512,1536]{1,0:T(8,128)S(1)} %get-tuple-element.189) | copy-start | bytes 9437188
  219.7 5.7 copy-start.15
  224.2 1.1 copy-start.11
  229.7 123.8 %all-gather.11.cloned.1.call-start = ((), (), s32[]{:S(2)}) async-start(), calls=%async_computation.8 | async-start | bytes 2359296 | tf_op jit(solution)/shard_map/all_gather | solution.py:135
  325.3 0.9 copy-start.3
  326.2 27.4 %copy-start.10 = (bf16[512,1536]{1,0:T(8,128)(2,1)S(1)}, bf16[512,1536]{1,0:T(8,128)(2,1)}, u32[]{:S(2)}) copy-start(bf16[512,1536]{1,0:T(8,128)(2,1)} %param.11) | copy-start | bytes 4718596
  326.2 251.7 %reduce-scatter.10.cloned.1.call-start = ((), (), s32[]{:S(2)}) async-start(), calls=%async_computation.9 | async-start | bytes 20054016 | tf_op jit(solution)/shard_map/reduce_scatter | solution.py:139
  353.5 4.3 copy-start
  383.6 1.1 copy-start.4
  383.7 3.4 copy-start.9
  387.1 190.8 %copy-start.1 = (bf16[96,1536]{1,0:T(8,128)(2,1)S(1)}, bf16[96,1536]{1,0:T(8,128)(2,1)}, u32[]{:S(2)}) copy-start(bf16[96,1536]{1,0:T(8,128)(2,1)} %param.14) | copy-start | bytes 884740
Sparse Core Ops, SparseCore 0:
  16.3 54.9 all-gather.4
  78.6 41.9 reduce-scatter.5
  123.4 53.1 all-gather.8
  178.6 25.7 all-gather.6
  229.8 44.5 reduce-scatter.7
  326.3 27.1 all-gather.10
  383.8 194.0 reduce-scatter.9
where the time goes:
time: 595 us; the launch traced here: 594 us
  waiting for transfers between devices  407 us (68%)
  matrix products  89.7 us (15%)
  local copies, waits for them, and re-layouts  37.6 us (6%)
  other arithmetic  26.8 us (5%)
  blocking collectives  17.7 us (3%)
  between operations  14.3 us (2%)
    reduce_scatter x1, waiting for transfers between devices, shards(): lax.psum_scatter(jnp.concatenate((contract_first(grad_values, hidden), co...  181 us
    all_gather x1, waiting for transfers between devices, shards(): lax.all_gather(unit_v.astype(jnp.bfloat16), 'fsdp', axis=0, tiled=True)  55 us
    reduce_scatter x1, waiting for transfers between devices, shards(): lax.psum_scatter(grad_attn_parts, 'grp', scatter_dimension=1, tiled=True)  44.7 us
    all_gather x1, waiting for transfers between devices, shards(): lax.all_gather(unit_o.astype(jnp.bfloat16), 'fsdp', axis=0, tiled=True)  40.5 us
    reduce_scatter x1, waiting for transfers between devices, shards(): lax.psum_scatter(value_parts, 'grp', scatter_dimension=1, tiled=True)  39 us
    dot_general x20, matrix products, contract_last(): lax.dot_general(left, right, (((1,), (1,)), ((), ())), preferred_element_...  28.7 us
    all_gather x1, waiting for transfers between devices, shards(): attn_all = lax.all_gather(attn_mine, 'grp', axis=1, tiled=True)  27.7 us
    dot_general x14, matrix products, contract_first(): lax.dot_general(left, right, (((0,), (0,)), ((), ())), preferred_element_...  27.4 us
  transfers between devices with their start and end apart: 7, of which 7 were waited for; matrix products, arithmetic and copies ran while one was open for 6% of the time, Pallas kernels for 0%

commit v1 on v0

--- a/solution.py
+++ b/solution.py
@@ -6,6 +6,11 @@
 D = 3072
 HS = 128
 EPS = 1e-06
+
+
+def tiled_gather(x, axis, dim):
+    copies = jnp.concatenate([x] * lax.axis_size(axis), axis=dim)
+    return lax.all_to_all(copies, axis, dim, dim, tiled=True)
 
 
 def contract_last(left, right):
@@ -77,7 +82,7 @@
     unit_o = out_rows / norm_o
     weight_v, weight_o = (
         lax.all_gather(unit_v.astype(jnp.bfloat16), "fsdp", axis=0, tiled=True),
-        lax.all_gather(unit_o.astype(jnp.bfloat16), "fsdp", axis=0, tiled=True),
+        tiled_gather(unit_o.astype(jnp.bfloat16), "fsdp", 0),
     )
     value_parts = contract_last(hidden, weight_v)
     values_mine = lax.psum_scatter(value_parts, "grp", scatter_dimension=1, tiled=True).astype(

time: 595 us -> 585 us (0.983)
  waiting for transfers between devices: 407 us -> 373 us
  other arithmetic: 26.8 us -> 42.3 us
    all_gather x1 -> x0, waiting for transfers between devices: 40.5 us -> none  [shards(): lax.all_gather(unit_o.astype(jnp.bfloat16), 'fsdp', axis=0, tiled=True)]
    all_to_all x0 -> x1, waiting for transfers between devices: none -> 39.6 us  [tiled_gather(): return lax.all_to_all(copies, axis, dim, dim, tiled=True)]
    all_gather x1, waiting for transfers between devices: 27.7 us -> 0.01 us  [shards(): attn_all = lax.all_gather(attn_mine, 'grp', axis=1, tiled=True)]
    unnamed x0 -> x15, other arithmetic: none -> 15.5 us
    reduce_scatter x1, waiting for transfers between devices: 44.7 us -> 59.6 us  [shards(): lax.psum_scatter(grad_attn_parts, 'grp', scatter_dimension=1, tiled=True)]
    all_gather x1, waiting for transfers between devices: 55 us -> 44.6 us  [shards(): lax.all_gather(unit_v.astype(jnp.bfloat16), 'fsdp', axis=0, tiled=True)]
    reduce_scatter x1, waiting for transfers between devices: 39 us -> 29.7 us  [shards(): lax.psum_scatter(value_parts, 'grp', scatter_dimension=1, tiled=True)]
  transfers between devices with their start and end apart: 7 -> 7, of which waited for: 7 -> 6; matrix products, arithmetic and copies ran while one was open for 6% -> 9% of each run, Pallas kernels for 0% -> 0%
where the time goes in v1:
time: 585 us; the launch traced here: 583 us
  waiting for transfers between devices  373 us (64%)
  matrix products  91.5 us (16%)
  other arithmetic  42.3 us (7%)
  local copies, waits for them, and re-layouts  37.1 us (6%)
  blocking collectives  19.1 us (3%)
  between operations  14.4 us (2%)
    reduce_scatter x1, waiting for transfers between devices, shards(): lax.psum_scatter(jnp.concatenate((contract_first(grad_values, hidden), co...  181 us
    reduce_scatter x1, waiting for transfers between devices, shards(): lax.psum_scatter(grad_attn_parts, 'grp', scatter_dimension=1, tiled=True)  59.6 us
    all_gather x1, waiting for transfers between devices, shards(): lax.all_gather(unit_v.astype(jnp.bfloat16), 'fsdp', axis=0, tiled=True)  44.6 us
    all_to_all x1, waiting for transfers between devices, tiled_gather(): return lax.all_to_all(copies, axis, dim, dim, tiled=True)  39.6 us
    dot_general x20, matrix products, contract_last(): lax.dot_general(left, right, (((1,), (1,)), ((), ())), preferred_element_...  30.5 us
    reduce_scatter x1, waiting for transfers between devices, shards(): lax.psum_scatter(value_parts, 'grp', scatter_dimension=1, tiled=True)  29.7 us
    dot_general x14, matrix products, contract_first(): lax.dot_general(left, right, (((0,), (0,)), ((), ())), preferred_element_...  27.4 us
    unnamed x37, local copies, waits for them, and re-layouts  26 us
  transfers between devices with their start and end apart: 7, of which 6 were waited for; matrix products, arithmetic and copies ran while one was open for 9% of the time, Pallas kernels for 0%

profile of v1, /device:TPU:0, one launch (start us, length us, event | category | flops | bytes accessed | tf_op | source)
XLA Modules:
  0.0 583.1 jit_solution(10828909652480373924)
XLA Ops:
  7.2 1.3 fusion.52
  8.5 6.0 %all-reduce.2 = (f32[96]{0:T(128)S(1)}, f32[96]{0:T(128)S(1)}) all-reduce(f32[96]{0:T(128)S(1)} %get-tuple-element.190, f32[96]{0:T(128)S(1)} %get-tuple-element.191), channel_id=1, replica_groups=mesh['fsdp'=16,'grp'=2] {'grp'}, use_global_device_ids=true, to_apply=%region_1.0 | all-reduce | flops 192 | bytes 1536 | tf_op jit(solution)/shard_map/psum | solution.py:76
  14.6 1.8 fusion.60
  16.4 1.8 constant_dynamic-update-slice_fusion.19
  18.2 1.8 constant_dynamic-update-slice_fusion.18
  20.0 1.8 constant_dynamic-update-slice_fusion.17
  26.9 44.6 %all-gather.4.cloned.1.call-done = bf16[1536,1536]{1,0:T(8,128)(2,1)} async-done(((bf16[96,1536]{1,0:T(8,128)(2,1)}), bf16[1536,1536]{1,0:T(8,128)(2,1)}) %all-gather.4.cloned.1.call-update) | async-done | bytes 4718608 | tf_op jit(solution)/shard_map/all_gather | solution.py:84
  71.5 6.6 %convolution_bitcast_fusion = f32[512,1536]{0,1:T(8,128)} fusion(bf16[1536,1536]{1,0:T(8,128)(2,1)} %all-gather.4.cloned.1.call-done, bf16[512,1536]{1,0:T(8,128)(2,1)S(1)} %copy-done.10), kind=kOutput, calls=%fused_computation.68 | convolution fusion | flops 2415919104 | bytes 9437184 | tf_op jit(solution)/shard_map/dot_general | solution.py:17
  84.1 4.7 all-to-all-start
  90.6 29.7 %reduce-scatter.6.cloned.1.call-done = f32[512,768]{0,1:T(8,128)} async-done(((f32[512,1536]{0,1:T(8,128)}), f32[512,768]{0,1:T(8,128)}) %reduce-scatter.6.cloned.1.call-update) | async-done | bytes 1572880 | tf_op jit(solution)/shard_map/reduce_scatter | solution.py:88
  120.3 1.5 convert_element_type.57
  123.1 11.8 %while.24 = (s32[]{:T(128)}, bf16[6,512,128]{1,2,0:T(8,128)(2,1)S(1)}, bf16[6,512,128]{2,1,0:T(8,128)(2,1)S(1)}, bf16[6,512,128]{2,1,0:T(8,128)(2,1)S(1)}, bf16[6,512,128]{2,1,0:T(8,128)(2,1)}, /*index=5*/s32[]{:T(128)}) while((s32[]{:T(128)}, bf16[6,512,128]{1,2,0:T(8,128)(2,1)S(1)}, bf16[6,512,128]{2,1,0:T(8,128)(2,1)S(1)}, ...), condition=%wide.region_6.7_spmd, body=%wide.region_3.6_spmd.sunk | while | flops 136641536 | bytes 4205653 | solution.py:94
  123.6 1.3 fusion.100
  125.5 1.3 fusion.100
  127.5 1.3 fusion.100
  129.5 1.3 fusion.100
  131.4 1.3 fusion.100
  133.4 1.3 fusion.100
  135.8 39.6 %all-to-all-done = bf16[16,96,1536]{2,1,0:T(8,128)(2,1)} async-done(((bf16[16,96,1536]{2,1,0:T(8,128)(2,1)}), bf16[16,96,1536]{2,1,0:T(8,128)(2,1)}, u32[]{:S(2)}, u32[]{:S(2)}) %all-to-all-start) | async-done | bytes 4718624 | tf_op jit(solution)/shard_map/all_to_all | solution.py:13
  175.4 8.4 %fusion.43 = (f32[512]{0:T(512)S(1)}, f32[512]{0:T(512)S(1)}, f32[512]{0:T(512)S(1)}, f32[512]{0:T(512)S(1)}, f32[512]{0:T(512)S(1)}, /*index=5*/f32[512]{0:T(512)S(1)}, f32[512,1536]{1,0:T(8,128)S(1)}) fusion(bf16[512,1536]{1,0:T(8,128)(2,1)} %param.17, f32[1536]{0:T(1024)S(1)} %copy-done.15, f32[1536]{0:T(1024)S(1)} %get-tuple-element.182, ...), kind=kOutput, calls=%fused_computation.72 | convolution fusion | flops 2430858240 | bytes 12625920 | tf_op jit(solution)/shard_map/dot_general | solution.py:96
  183.8 8.1 %all-reduce.1 = (f32[512]{0:T(512)S(1)}, f32[512]{0:T(512)S(1)}, f32[512]{0:T(512)S(1)}, f32[512]{0:T(512)S(1)}, f32[512]{0:T(512)S(1)}, /*index=5*/f32[512]{0:T(512)S(1)}) all-reduce(f32[512]{0:T(512)S(1)} %get-tuple-element.126, f32[512]{0:T(512)S(1)} %get-tuple-element.130, ...), channel_id=1, replica_groups=mesh['fsdp'=16,'grp'=2] {'grp'}, use_global_device_ids=true, to_apply=%region_16.17 | all-reduce | flops 3072 | bytes 24576 | tf_op jit(solution)/shard_map/psum | solution.py:99
  192.0 4.4 multiply_convert_fusion.1
  197.5 6.6 %fusion.65 = f32[512,1536]{1,0:T(8,128)} fusion(bf16[512,1536]{1,0:T(8,128)(2,1)S(1)} %get-tuple-element.177, bf16[1536,1536]{1,0:T(8,128)(2,1)} %bitcast.21), kind=kOutput, calls=%fused_computation.128 | convolution fusion | flops 2415919104 | bytes 9437184 | tf_op jit(solution)/shard_map/dot_general | solution.py:17
  204.2 59.6 %reduce-scatter.8.cloned.1.call-done = f32[512,768]{1,0:T(8,128)} async-done(((f32[512,1536]{1,0:T(8,128)}), f32[512,768]{1,0:T(8,128)}) %reduce-scatter.8.cloned.1.call-update) | async-done | bytes 1572880 | tf_op jit(solution)/shard_map/reduce_scatter | solution.py:134
  263.8 1.5 convert_element_type.63
  267.5 47.0 %while.25 = (s32[]{:T(128)}, bf16[6,512,128]{1,2,0:T(8,128)(2,1)}, bf16[6,512,128]{1,2,0:T(8,128)(2,1)S(1)}, bf16[6,512,128]{1,2,0:T(8,128)(2,1)S(1)}, bf16[6,51...) while((s32[]{:T(128)}, bf16[6,512,128]{1,2,0:T(8,128)(2,1)}, ...), condition=%wide.region_26.27_spmd, body=%wide.region_22.26_spmd.sunk | while | flops 340589056 | bytes 11821177 | solution.py:137
  267.5 1.3 fusion.107
  270.4 1.3 multiply_reduce_fusion.5
  275.4 1.3 fusion.107
  278.2 1.3 multiply_reduce_fusion.5
  283.2 1.3 fusion.107
  286.1 1.3 multiply_reduce_fusion.5
  291.0 1.3 fusion.107
  293.9 1.3 multiply_reduce_fusion.5
  298.9 1.3 fusion.107
  301.7 1.3 multiply_reduce_fusion.5
  306.7 1.3 fusion.107
  309.6 1.3 multiply_reduce_fusion.5
  315.5 8.5 %fusion.67 = f32[1536,1536]{0,1:T(8,128)} fusion(bf16[512,1536]{0,1:T(8,128)(2,1)} %all-gather.6.cloned.1.call-done, bf16[512,1536]{1,0:T(8,128)(2,1)} %copy-done.12), kind=kOutput, calls=%fused_computation.130 | convolution fusion | flops 2415919104 | bytes 12582912 | tf_op jit(solution)/shard_map/dot_general | solution.py:23
  324.0 18.8 %all-gather.8.cloned.1.call-done = bf16[512,1536]{0,1:T(8,128)(2,1)} async-done(((bf16[512,768]{0,1:T(8,128)(2,1)}), bf16[512,1536]{0,1:T(8,128)(2,1)}) %all-gather.8.cloned.1.call-update) | async-done | bytes 1572880 | tf_op jit(solution)/shard_map/all_gather | solution.py:140
  342.8 4.2 fusion.66
  347.1 7.2 %pad_maximum_fusion = f32[1536,3072]{0,1:T(8,128)} fusion(f32[1536,1536]{0,1:T(8,128)S(1)} %copy-done.1, f32[1536,1536]{0,1:T(8,128)S(1)} %fusion.66), kind=kLoop, calls=%fused_computation.57 | loop fusion | flops 4718592 | bytes 37748736 | tf_op jit(solution)/shard_map/concatenate | solution.py:145
  354.3 18.7 %copy.58 = f32[1536,3072]{1,0:T(8,128)} copy(f32[1536,3072]{0,1:T(8,128)} %pad_maximum_fusion) | data formatting | bytes 37748736
  376.4 10.0 %fusion.51 = bf16[512,1536]{1,0:T(8,128)(2,1)} fusion(bf16[512,1536]{0,1:T(8,128)(2,1)} %all-gather.8.cloned.1.call-done, bf16[1536,1536]{1,0:T(8,128)(2,1)} %all-gather.4.cloned.1.call-done, bf16[512,1536]{1,0:T(8,128)(2,1)S(1)} %copy-done.9, f32[512]{0:T(512)S(1)} %get-tuple-element.187, f32[1536]{0:T(1024)S(1)} %get-tuple-element.185, ...), kind=kOutput, calls=%fused_computation.82 | convolution fusion | flops 2426929152 | bytes 14174208 | tf_op jit(solution)/shard_map/dot_general | solution.py:142
  386.4 180.8 %reduce-scatter.10.cloned.1.call-done = f32[96,3072]{1,0:T(8,128)} async-done(((f32[1536,3072]{1,0:T(8,128)}), f32[96,3072]{1,0:T(8,128)}) %reduce-scatter.10.cloned.1.call-update) | async-done | bytes 1179664 | tf_op jit(solution)/shard_map/reduce_scatter | solution.py:144
  567.2 1.6 multiply_reduce_fusion.2
  568.8 4.9 all-reduce
  573.7 2.5 subtract_divide_fusion
  (158 shorter events, 58.1 us)
Async XLA Ops:
  7.2 14.7 %copy-start = (bf16[96,1536]{1,0:T(8,128)(2,1)S(1)}, bf16[96,1536]{1,0:T(8,128)(2,1)}, u32[]{:S(2)}) copy-start(bf16[96,1536]{1,0:T(8,128)(2,1)} %param.15) | copy-start | bytes 884740
  7.2 64.3 %all-gather.4.cloned.1.call-start = ((), (), s32[]{:S(2)}) async-start(), calls=%async_computation.4 | async-start | bytes 5013504 | tf_op jit(solution)/shard_map/all_gather | solution.py:84
  8.5 63.0 %copy-start.10 = (bf16[512,1536]{1,0:T(8,128)(2,1)S(1)}, bf16[512,1536]{1,0:T(8,128)(2,1)}, u32[]{:S(2)}) copy-start(bf16[512,1536]{1,0:T(8,128)(2,1)} %param.11) | copy-start | bytes 4718596
  16.4 103.9 %reduce-scatter.6.cloned.1.call-start = ((), (), s32[]{:S(2)}) async-start(), calls=%async_computation.5 | async-start | bytes 4718592 | tf_op jit(solution)/shard_map/reduce_scatter | solution.py:88
  84.1 4.8 copy-start.13
  84.1 91.3 %all-to-all-start = ((bf16[16,96,1536]{2,1,0:T(8,128)(2,1)}), bf16[16,96,1536]{2,1,0:T(8,128)(2,1)}, u32[]{:S(2)}, u32[]{:S(2)}) async-start(bf16[16,96,1536]{2,1,0:T(8,128)(2,1)} %bitcast.20), calls=%async_computation.1 | async-start | bytes 9437184 | tf_op jit(solution)/shard_map/all_to_all | solution.py:13
  88.8 1.1 copy-start.14
  88.8 86.6 %all-gather.6.cloned.1.call-start = ((), (), s32[]{:S(2)}) async-start(), calls=%async_computation.6 | async-start | bytes 2359296 | tf_op jit(solution)/shard_map/all_gather | solution.py:95
  123.0 12.7 %copy-start.15 = (f32[1536]{0:T(1024)S(1)}, f32[1536]{0:T(1024)}, u32[]{:S(2)}) copy-start(f32[1536]{0:T(1024)} %param.16) | copy-start | bytes 18436
  134.8 0.9 copy-start.5
  134.8 40.6 %copy-start.7 = (bf16[6,512,128]{2,1,0:T(8,128)(2,1)}, bf16[6,512,128]{2,1,0:T(8,128)(2,1)S(1)}, u32[]{:S(2)}) copy-start(bf16[6,512,128]{2,1,0:T(8,128)(2,1)S(1)} %get-tuple-element.350) | copy-start | bytes 2359300
  134.8 40.6 %copy-start.8 = (bf16[6,512,128]{2,1,0:T(8,128)(2,1)}, bf16[6,512,128]{2,1,0:T(8,128)(2,1)S(1)}, u32[]{:S(2)}) copy-start(bf16[6,512,128]{2,1,0:T(8,128)(2,1)S(1)} %get-tuple-element.351) | copy-start | bytes 2359300
  135.7 128.1 %reduce-scatter.8.cloned.1.call-start = ((), (), s32[]{:S(2)}) async-start(), calls=%async_computation.7 | async-start | bytes 4718592 | tf_op jit(solution)/shard_map/reduce_scatter | solution.py:134
  183.8 12.5 %copy-start.6 = (f32[512,1536]{1,0:T(8,128)}, f32[512,1536]{1,0:T(8,128)S(1)}, u32[]{:S(2)}) copy-start(f32[512,1536]{1,0:T(8,128)S(1)} %get-tuple-element.189) | copy-start | bytes 9437188
  196.4 1.1 copy-start.12
  204.2 138.7 %all-gather.8.cloned.1.call-start = ((), (), s32[]{:S(2)}) async-start(), calls=%async_computation.8 | async-start | bytes 2359296 | tf_op jit(solution)/shard_map/all_gather | solution.py:140
  314.6 0.9 copy-start.3
  315.5 27.4 %copy-start.11 = (bf16[512,1536]{1,0:T(8,128)(2,1)S(1)}, bf16[512,1536]{1,0:T(8,128)(2,1)}, u32[]{:S(2)}) copy-start(bf16[512,1536]{1,0:T(8,128)(2,1)} %param.11) | copy-start | bytes 4718596
  315.5 251.7 %reduce-scatter.10.cloned.1.call-start = ((), (), s32[]{:S(2)}) async-start(), calls=%async_computation.9 | async-start | bytes 20054016 | tf_op jit(solution)/shard_map/reduce_scatter | solution.py:144
  342.8 4.3 copy-start.1
  372.9 1.1 copy-start.4
  373.0 3.4 copy-start.9
  376.4 190.8 %copy-start.2 = (bf16[96,1536]{1,0:T(8,128)(2,1)S(1)}, bf16[96,1536]{1,0:T(8,128)(2,1)}, u32[]{:S(2)}) copy-start(bf16[96,1536]{1,0:T(8,128)(2,1)} %param.14) | copy-start | bytes 884740
Sparse Core Ops, SparseCore 0:
  16.5 54.9 all-gather.3
  78.2 42.0 reduce-scatter.5
  135.8 27.1 all-gather.5
  204.3 59.4 reduce-scatter.7
  315.6 27.1 all-gather.7
  373.1 194.0 reduce-scatter.9
